TPU v7x, 32 devices: a whole 2x2x4 slice. The times are simulated.
32 devices in a mesh: expert: 4 (over y, core), fsdp: 8 (over z, x).
Axes of the slice: x: 2, y: 2, z: 4, core: 2. Of those that a mesh axis runs over, the one named last changes fastest.
Arguments:
- gradients: bfloat16 [8, 3584, 1024], P('expert', 'fsdp'), may hold values from -24 to 24, as said below
- owner: int32 [4, 2], P('expert'), may hold values from 0 to 1, each once within a row
Outputs:
- updates: bfloat16 [8, 3584, 1024], P('expert', 'fsdp')
- slot_rms: float32 [4, 8], P('expert', 'fsdp')
Inputs may be any that keep to these rules, and one draw needn't show every extreme that they name: gradients are values of mean zero and unit variance times a factor per expert between 0.5 and 2 and a factor per expert and row slice between 0.5 and 2, each entry within 24 in magnitude. Each row of owner names every place 0 to 1 exactly once.
All inputs are finite; a program needn't handle non-finite values.
Results may differ from a plain program's by a relative error of at most 0.009.
Values may be sent and summed in bfloat16 or wider, within the bound.
A program may use at most 64 MiB of HBM per device.

v0:
```python
import math

import jax
import jax.numpy as jnp
from jax import lax
from jax.sharding import PartitionSpec as P

ROWS = 3584
COLS = 1024
SHARE = 4
ITERS = 3


coef_a = 3.4445
coef_b = -4.775
coef_c = 2.0315
epsilon = 1e-07


def as_sent(value):
    return jax.tree.map(lambda a: a.astype(jnp.bfloat16) if a.dtype == jnp.float32 else a, value)


def partner_2(value, axis, distance):
    mask = 2**distance
    pairs = [(source, source ^ mask) for source in range(lax.axis_size(axis))]
    return lax.ppermute(value, axis, pairs)


def select_half(stacked, bit_value):
    retained = lax.dynamic_index_in_dim(stacked, bit_value, 0, keepdims=False)
    outgoing = lax.dynamic_index_in_dim(stacked, 1 - bit_value, 0, keepdims=False)
    return (retained, outgoing)


def join_halves(own_block, theirs, bit_value):
    leading = jnp.where(bit_value == 0, own_block, theirs)
    trailing = jnp.where(bit_value == 0, theirs, own_block)
    return jnp.concatenate([leading, trailing], axis=0)


def reduce_gram(current, low_bit, high_bit):
    partial_gram = lax.dot_general(
        current, current, (((0,), (0,)), ((), ())), preferred_element_type=jnp.float32
    )
    rounded = lax.optimization_barrier(partial_gram.astype(jnp.bfloat16))
    columns = rounded.shape[1]
    retained, outgoing = select_half(rounded.reshape(2, columns // 2, columns), low_bit)
    arrived = partner_2(as_sent(outgoing), "fsdp", 0).astype(outgoing.dtype)
    pair_sum = retained.astype(jnp.float32) + arrived.astype(jnp.float32)
    retained_pair, outgoing_pair = select_half(pair_sum.reshape(2, columns // 4, columns), high_bit)
    arrived_pair = partner_2(as_sent(outgoing_pair), "fsdp", 1).astype(outgoing_pair.dtype)
    return (retained_pair + arrived_pair).astype(jnp.bfloat16)


def spread_gram(quarter, low_bit, high_bit):
    incoming = partner_2(quarter, "fsdp", 1)
    half_block = join_halves(quarter, incoming, high_bit)
    partner = partner_2(as_sent(half_block), "fsdp", 0).astype(half_block.dtype)
    return join_halves(half_block, partner, low_bit)


def body(gradients, owner):
    expert_count, local_rows, columns = gradients.shape
    fsdp_index = lax.axis_index("fsdp")
    low_bit = fsdp_index % 2
    high_bit = fsdp_index // 2 % 2
    owner_row = owner[0]
    places = jnp.arange(expert_count, dtype=jnp.int32)
    inverse = jnp.sum(
        jnp.where(owner_row[None, :] == places[:, None], places[None, :], 0), axis=1
    ).astype(jnp.int32)
    expert_sums = jnp.sum(jnp.square(gradients.astype(jnp.float32)), axis=(1, 2))
    totals = lax.psum(expert_sums, "fsdp")
    own_expert = lax.dynamic_index_in_dim(inverse, fsdp_index // SHARE, 0, keepdims=False)
    square_sum = lax.dynamic_index_in_dim(totals, own_expert, 0, keepdims=False)
    ordered = jnp.take(gradients, inverse, axis=0)
    outbound = ordered.reshape(expert_count * SHARE, local_rows // SHARE, columns)
    held = lax.all_to_all(outbound, "fsdp", split_axis=0, concat_axis=1, tiled=True)[0]
    norm_value = jnp.sqrt(square_sum)
    current = (held.astype(jnp.float32) / (norm_value + epsilon)).astype(jnp.bfloat16)
    for iteration in range(ITERS):
        quarter = reduce_gram(current, low_bit, high_bit)
        gram_full = spread_gram(quarter, low_bit, high_bit)
        squared = jnp.dot(gram_full, gram_full, preferred_element_type=jnp.float32)
        poly = (coef_b * gram_full.astype(jnp.float32) + coef_c * squared).astype(jnp.bfloat16)
        current = (
            coef_a * current.astype(jnp.float32)
            + jnp.dot(current, poly, preferred_element_type=jnp.float32)
        ).astype(jnp.bfloat16)
    update = (math.sqrt(ROWS) * current.astype(jnp.float32)).astype(jnp.bfloat16)
    returned = lax.all_to_all(update[None], "fsdp", split_axis=1, concat_axis=0, tiled=True)
    slot_order = returned.reshape(expert_count, local_rows, columns)
    updates = jnp.take(slot_order, owner_row, axis=0)
    slot_rms = (norm_value / math.sqrt(ROWS * COLS)).reshape(1, 1).astype(jnp.float32)
    return (updates, slot_rms)


def solution(mesh):
    placed = (P("expert", "fsdp", None), P("expert", None))
    return jax.shard_map(
        body,
        mesh=mesh,
        in_specs=placed,
        out_specs=(P("expert", "fsdp", None), P("expert", "fsdp")),
        check_vma=False,
    )
```

profile of v0, /device:TPU:0, one launch (start us, length us, event | category | flops | bytes accessed | tf_op | source)
XLA Modules:
  0.0 335.4 jit_solution(16962302694401268506)
XLA Ops:
  0.6 0.8 fusion.16
  1.4 0.7 compare_select_fusion
  2.1 0.7 compare_and_fusion
  2.7 2.2 gather_fusion
  4.9 1.5 broadcast_select_fusion.1
  6.4 7.3 %all-to-all-start = ((bf16[8,112,1024]{2,1,0:T(8,128)(2,1)}), bf16[8,112,1024]{2,1,0:T(8,128)(2,1)S(1)}, u32[]{:S(2)}, u32[]{:S(2)}) async-start(bf16[8,112,1024]{2,1,0:T(8,128)(2,1)} %bitcast.71), calls=%async_computation | async-start | bytes 3670016 | tf_op jit(solution)/shard_map/all_to_all | solution.py:79
  13.7 2.1 multiply_reduce_fusion
  15.8 43.5 %psum.7 = f32[2]{0:T(128)S(1)} all-reduce(f32[2]{0:T(128)S(1)} %multiply_reduce_fusion), channel_id=1, replica_groups=mesh['expert'=4,'fsdp'=8] {'fsdp'}, use_global_device_ids=true, to_apply=%region_2.4 | all-reduce | flops 2 | bytes 16 | tf_op jit(solution)/shard_map/psum | solution.py:74
  59.3 0.6 dynamic_slice.46
  61.9 0.6 dynamic_slice.47
  63.2 0.4 divide_convert_fusion
  63.6 2.4 bitcast_convert_fusion
  66.0 1.3 copy-done
  67.4 5.5 %collective-permute-start = (bf16[512,1024]{1,0:T(8,128)(2,1)S(1)}, bf16[512,1024]{1,0:T(8,128)(2,1)S(1)}, u32[]{:S(2)}, u32[]{:S(2)}) collective-permute-start(bf16[512,1024]{1,0:T(8,128)(2,1)S(1)} %dynamic-slice_bitcast_fusion.2), channel_id=1, source_target_pairs={{0,1},{1,0},{2,3},{3,2},{4,5},{5,4},{6,7},{7,6},{8,9},{9,8},{10,11... | collective-permute-start | bytes 3145736 | tf_op jit(solution)/shard_map/ppermute | solution.py:27
  72.9 19.1 %collective-permute-done = bf16[512,1024]{1,0:T(8,128)(2,1)S(1)} collective-permute-done((bf16[512,1024]{1,0:T(8,128)(2,1)S(1)}, bf16[512,1024]{1,0:T(8,128)(2,1)S(1)}, u32[]{:S(2)}, u32[]{:S(2)}) %collective-permute-start) | collective-permute-done | bytes 1048608 | tf_op jit(solution)/shard_map/ppermute | solution.py:27
  92.0 1.6 convert_add_fusion.2
  93.6 0.1 fusion.13
  93.7 3.3 collective-permute-start.1
  97.0 10.2 %collective-permute-done.1 = bf16[256,1024]{1,0:T(8,128)(2,1)S(1)} collective-permute-done((bf16[256,1024]{1,0:T(8,128)(2,1)S(1)}, bf16[256,1024]{1,0:T(8,128)(2,1)S(1)}, u32[]{:S(2)}, u32[]{:S(2)}) %collective-permute-start.1) | collective-permute-done | bytes 524320 | tf_op jit(solution)/shard_map/ppermute | solution.py:27
  107.1 0.1 fusion.12
  107.3 2.4 collective-permute-start.2
  109.7 7.2 %collective-permute-done.2 = bf16[256,1024]{1,0:T(8,128)(2,1)S(1)} collective-permute-done((bf16[256,1024]{1,0:T(8,128)(2,1)S(1)}, bf16[256,1024]{1,0:T(8,128)(2,1)S(1)}, u32[]{:S(2)}, u32[]{:S(2)}) %collective-permute-start.2) | collective-permute-done | bytes 524320 | tf_op jit(solution)/shard_map/ppermute | solution.py:27
  117.0 1.2 collective-permute-start.3
  118.2 17.4 %collective-permute-done.3 = bf16[512,1024]{1,0:T(8,128)(2,1)S(1)} collective-permute-done((bf16[512,1024]{1,0:T(8,128)(2,1)S(1)}, bf16[512,1024]{1,0:T(8,128)(2,1)S(1)}, u32[]{:S(2)}, u32[]{:S(2)}) %collective-permute-start.3) | collective-permute-done | bytes 1048608 | tf_op jit(solution)/shard_map/ppermute | solution.py:27
  135.6 0.5 broadcast_select_fusion.7
  136.2 2.5 add_convert_fusion.2
  138.6 2.1 add_convert_fusion.5
  140.7 2.4 convolution_convert_fusion.1
  143.2 1.8 collective-permute-start.4
  145.0 16.6 %collective-permute-done.4 = bf16[512,1024]{1,0:T(8,128)(2,1)S(1)} collective-permute-done((bf16[512,1024]{1,0:T(8,128)(2,1)S(1)}, bf16[512,1024]{1,0:T(8,128)(2,1)S(1)}, u32[]{:S(2)}, u32[]{:S(2)}) %collective-permute-start.4) | collective-permute-done | bytes 1048608 | tf_op jit(solution)/shard_map/ppermute | solution.py:27
  161.6 0.4 convert_add_fusion.1
  162.1 1.5 collective-permute-start.5
  163.6 13.0 %collective-permute-done.5 = bf16[256,1024]{1,0:T(8,128)(2,1)S(1)} collective-permute-done((bf16[256,1024]{1,0:T(8,128)(2,1)S(1)}, bf16[256,1024]{1,0:T(8,128)(2,1)S(1)}, u32[]{:S(2)}, u32[]{:S(2)}) %collective-permute-start.5) | collective-permute-done | bytes 524320 | tf_op jit(solution)/shard_map/ppermute | solution.py:27
  176.6 0.2 fusion.11
  176.8 1.2 collective-permute-start.6
  178.0 8.0 %collective-permute-done.6 = bf16[256,1024]{1,0:T(8,128)(2,1)S(1)} collective-permute-done((bf16[256,1024]{1,0:T(8,128)(2,1)S(1)}, bf16[256,1024]{1,0:T(8,128)(2,1)S(1)}, u32[]{:S(2)}, u32[]{:S(2)}) %collective-permute-start.6) | collective-permute-done | bytes 524320 | tf_op jit(solution)/shard_map/ppermute | solution.py:27
  186.2 1.8 collective-permute-start.7
  188.0 13.7 %collective-permute-done.7 = bf16[512,1024]{1,0:T(8,128)(2,1)S(1)} collective-permute-done((bf16[512,1024]{1,0:T(8,128)(2,1)S(1)}, bf16[512,1024]{1,0:T(8,128)(2,1)S(1)}, u32[]{:S(2)}, u32[]{:S(2)}) %collective-permute-start.7) | collective-permute-done | bytes 1048608 | tf_op jit(solution)/shard_map/ppermute | solution.py:27
  201.7 0.6 broadcast_select_fusion.5
  202.3 2.7 add_convert_fusion.1
  205.0 2.1 add_convert_fusion.4
  207.1 2.4 convolution_convert_fusion
  209.6 1.8 collective-permute-start.8
  211.4 13.1 %collective-permute-done.8 = bf16[512,1024]{1,0:T(8,128)(2,1)S(1)} collective-permute-done((bf16[512,1024]{1,0:T(8,128)(2,1)S(1)}, bf16[512,1024]{1,0:T(8,128)(2,1)S(1)}, u32[]{:S(2)}, u32[]{:S(2)}) %collective-permute-start.8) | collective-permute-done | bytes 1048608 | tf_op jit(solution)/shard_map/ppermute | solution.py:27
  224.4 0.4 convert_add_fusion
  224.9 1.2 collective-permute-start.9
  226.1 9.7 %collective-permute-done.9 = bf16[256,1024]{1,0:T(8,128)(2,1)S(1)} collective-permute-done((bf16[256,1024]{1,0:T(8,128)(2,1)S(1)}, bf16[256,1024]{1,0:T(8,128)(2,1)S(1)}, u32[]{:S(2)}, u32[]{:S(2)}) %collective-permute-start.9) | collective-permute-done | bytes 524320 | tf_op jit(solution)/shard_map/ppermute | solution.py:27
  235.8 0.2 fusion.10
  235.9 0.9 collective-permute-start.10
  236.8 8.3 %collective-permute-done.10 = bf16[256,1024]{1,0:T(8,128)(2,1)S(1)} collective-permute-done((bf16[256,1024]{1,0:T(8,128)(2,1)S(1)}, bf16[256,1024]{1,0:T(8,128)(2,1)S(1)}, u32[]{:S(2)}, u32[]{:S(2)}) %collective-permute-start.10) | collective-permute-done | bytes 524320 | tf_op jit(solution)/shard_map/ppermute | solution.py:27
  245.3 1.8 collective-permute-start.11
  247.1 13.1 %collective-permute-done.11 = bf16[512,1024]{1,0:T(8,128)(2,1)S(1)} collective-permute-done((bf16[512,1024]{1,0:T(8,128)(2,1)S(1)}, bf16[512,1024]{1,0:T(8,128)(2,1)S(1)}, u32[]{:S(2)}, u32[]{:S(2)}) %collective-permute-start.11) | collective-permute-done | bytes 1048608 | tf_op jit(solution)/shard_map/ppermute | solution.py:27
  260.2 1.5 broadcast_select_fusion.3
  261.7 7.5 %fusion.9 = bf16[1,896,1024]{2,1,0:T(8,128)(2,1)S(1)} fusion(bf16[896,1024]{1,0:T(8,128)(2,1)} %copy-done.3, bf16[512,1024]{1,0:T(8,128)(2,1)} %get-tuple-element.4, bf16[512,1024]{1,0:T(8,128)(2,1)S(1)} %get-tuple-element.3), kind=kOutput, calls=%fused_computation.26 | convolution fusion | flops 4045537280 | bytes 5767168 | tf_op jit(solution)/shard_map/dot_general | solution.py:89
  269.3 4.8 %copy.9 = bf16[1,896,1024]{2,0,1:T(2,128)(2,1)} copy(bf16[1,896,1024]{2,1,0:T(8,128)(2,1)S(1)} %fusion.9) | data formatting | bytes 3670016 | tf_op jit(solution)/shard_map/broadcast_in_dim | solution.py:92
  274.1 0.5 broadcast.84
  274.6 11.4 %reduce = bf16[896,1024]{1,0:T(8,128)(2,1)S(1)} reduce(bf16[896,1,1024]{2,1,0:T(2,128)(2,1)} %bitcast.69, bf16[]{:T(256)} %broadcast.84), dimensions={1}, to_apply=%bitcast.68.reduce_sub_computation | reduce | bytes 3670018
  286.0 3.7 %reshape.106 = bf16[8,2,57344]{2,1,0:T(2,128)(2,1)} reshape(bf16[896,1024]{1,0:T(8,128)(2,1)S(1)} %reduce) | data formatting | bytes 3670016
  289.7 4.2 %all-to-all-start.1 = ((bf16[8,2,57344]{2,1,0:T(2,128)(2,1)}), bf16[8,2,57344]{2,1,0:T(2,128)(2,1)S(1)}, u32[]{:S(2)}, u32[]{:S(2)}) async-start(bf16[8,2,57344]{2,1,0:T(2,128)(2,1)} %reshape.106), calls=%async_computation.1 | async-start | bytes 3670016 | tf_op jit(solution)/shard_map/all_to_all | solution.py:92
  293.9 28.7 %all-to-all-done.1 = bf16[8,2,57344]{2,1,0:T(2,128)(2,1)S(1)} async-done(((bf16[8,2,57344]{2,1,0:T(2,128)(2,1)}), bf16[8,2,57344]{2,1,0:T(2,128)(2,1)S(1)}, u32[]{:S(2)}, u32[]{:S(2)}) %all-to-all-start.1) | async-done | bytes 1835040 | tf_op jit(solution)/shard_map/all_to_all | solution.py:92
  322.5 4.1 %reshape.107 = bf16[896,1,1024]{2,1,0:T(2,128)(2,1)} reshape(bf16[8,2,57344]{2,1,0:T(2,128)(2,1)S(1)} %all-to-all-done.1) | data formatting | bytes 3670016
  326.7 4.0 %copy.7 = bf16[1,896,1024]{2,1,0:T(8,128)(2,1)} copy(bf16[1,896,1024]{2,0,1:T(2,128)(2,1)} %bitcast.70) | data formatting | bytes 3670016
  330.7 2.2 gather_fusion.1
  332.8 1.5 broadcast_select_fusion
  (21 shorter events, 0.8 us)
Async XLA Ops:
  6.4 56.8 %all-to-all-start = ((bf16[8,112,1024]{2,1,0:T(8,128)(2,1)}), bf16[8,112,1024]{2,1,0:T(8,128)(2,1)S(1)}, u32[]{:S(2)}, u32[]{:S(2)}) async-start(bf16[8,112,1024]{2,1,0:T(8,128)(2,1)} %bitcast.71), calls=%async_computation | async-start | bytes 3670016 | tf_op jit(solution)/shard_map/all_to_all | solution.py:79
  63.6 2.4 copy-start.1
  66.0 1.3 copy-start
  67.4 24.6 %collective-permute-start = (bf16[512,1024]{1,0:T(8,128)(2,1)S(1)}, bf16[512,1024]{1,0:T(8,128)(2,1)S(1)}, u32[]{:S(2)}, u32[]{:S(2)}) collective-permute-start(bf16[512,1024]{1,0:T(8,128)(2,1)S(1)} %dynamic-slice_bitcast_fusion.2), channel_id=1, source_target_pairs={{0,1},{1,0},{2,3},{3,2},{4,5},{5,4},{6,7},{7,6},{8,9},{9,8},{10,11... | collective-permute-start | bytes 3145736 | tf_op jit(solution)/shard_map/ppermute | solution.py:27
  93.7 13.5 %collective-permute-start.1 = (bf16[256,1024]{1,0:T(8,128)(2,1)S(1)}, bf16[256,1024]{1,0:T(8,128)(2,1)S(1)}, u32[]{:S(2)}, u32[]{:S(2)}) collective-permute-start(bf16[256,1024]{1,0:T(8,128)(2,1)S(1)} %fusion.13), channel_id=1, source_target_pairs={{0,2},{1,3},{2,0},{3,1},{4,6},{5,7},{6,4},{7,5},{8,10},{9,11},{10,... | collective-permute-start | bytes 1572872 | tf_op jit(solution)/shard_map/ppermute | solution.py:27
  107.3 9.5 %collective-permute-start.2 = (bf16[256,1024]{1,0:T(8,128)(2,1)S(1)}, bf16[256,1024]{1,0:T(8,128)(2,1)S(1)}, u32[]{:S(2)}, u32[]{:S(2)}) collective-permute-start(bf16[256,1024]{1,0:T(8,128)(2,1)S(1)} %fusion.12), channel_id=1, source_target_pairs={{0,2},{1,3},{2,0},{3,1},{4,6},{5,7},{6,4},{7,5},{8,10},{9,11},{10,... | collective-permute-start | bytes 1572872 | tf_op jit(solution)/shard_map/ppermute | solution.py:27
  117.0 18.6 %collective-permute-start.3 = (bf16[512,1024]{1,0:T(8,128)(2,1)S(1)}, bf16[512,1024]{1,0:T(8,128)(2,1)S(1)}, u32[]{:S(2)}, u32[]{:S(2)}) collective-permute-start(bf16[512,1024]{1,0:T(8,128)(2,1)S(1)} %pad_maximum_fusion), channel_id=1, source_target_pairs={{0,1},{1,0},{2,3},{3,2},{4,5},{5,4},{6,7},{7,6},{8,9},{9,8},{10,11... | collective-permute-start | bytes 3145736 | tf_op jit(solution)/shard_map/ppermute | solution.py:27
  136.2 2.5 copy-start.2
  143.2 18.4 %collective-permute-start.4 = (bf16[512,1024]{1,0:T(8,128)(2,1)S(1)}, bf16[512,1024]{1,0:T(8,128)(2,1)S(1)}, u32[]{:S(2)}, u32[]{:S(2)}) collective-permute-start(bf16[512,1024]{1,0:T(8,128)(2,1)S(1)} %dynamic-slice_bitcast_fusion.1), channel_id=1, source_target_pairs={{0,1},{1,0},{2,3},{3,2},{4,5},{5,4},{6,7},{7,6},{8,9},{9,8},{10,11... | collective-permute-start | bytes 3145736 | tf_op jit(solution)/shard_map/ppermute | solution.py:27
  162.1 14.6 %collective-permute-start.5 = (bf16[256,1024]{1,0:T(8,128)(2,1)S(1)}, bf16[256,1024]{1,0:T(8,128)(2,1)S(1)}, u32[]{:S(2)}, u32[]{:S(2)}) collective-permute-start(bf16[256,1024]{1,0:T(8,128)(2,1)S(1)} %fusion.14), channel_id=1, source_target_pairs={{0,2},{1,3},{2,0},{3,1},{4,6},{5,7},{6,4},{7,5},{8,10},{9,11},{10,... | collective-permute-start | bytes 1572872 | tf_op jit(solution)/shard_map/ppermute | solution.py:27
  176.8 9.2 %collective-permute-start.6 = (bf16[256,1024]{1,0:T(8,128)(2,1)S(1)}, bf16[256,1024]{1,0:T(8,128)(2,1)S(1)}, u32[]{:S(2)}, u32[]{:S(2)}) collective-permute-start(bf16[256,1024]{1,0:T(8,128)(2,1)S(1)} %fusion.11), channel_id=1, source_target_pairs={{0,2},{1,3},{2,0},{3,1},{4,6},{5,7},{6,4},{7,5},{8,10},{9,11},{10,... | collective-permute-start | bytes 1572872 | tf_op jit(solution)/shard_map/ppermute | solution.py:27
  186.2 15.5 %collective-permute-start.7 = (bf16[512,1024]{1,0:T(8,128)(2,1)S(1)}, bf16[512,1024]{1,0:T(8,128)(2,1)S(1)}, u32[]{:S(2)}, u32[]{:S(2)}) collective-permute-start(bf16[512,1024]{1,0:T(8,128)(2,1)S(1)} %pad_maximum_fusion.1), channel_id=1, source_target_pairs={{0,1},{1,0},{2,3},{3,2},{4,5},{5,4},{6,7},{7,6},{8,9},{9,8},{10,11... | collective-permute-start | bytes 3145736 | tf_op jit(solution)/shard_map/ppermute | solution.py:27
  207.1 2.4 copy-start.3
  209.6 14.9 %collective-permute-start.8 = (bf16[512,1024]{1,0:T(8,128)(2,1)S(1)}, bf16[512,1024]{1,0:T(8,128)(2,1)S(1)}, u32[]{:S(2)}, u32[]{:S(2)}) collective-permute-start(bf16[512,1024]{1,0:T(8,128)(2,1)S(1)} %dynamic-slice_bitcast_fusion), channel_id=1, source_target_pairs={{0,1},{1,0},{2,3},{3,2},{4,5},{5,4},{6,7},{7,6},{8,9},{9,8},{10,11... | collective-permute-start | bytes 3145736 | tf_op jit(solution)/shard_map/ppermute | solution.py:27
  224.9 10.8 %collective-permute-start.9 = (bf16[256,1024]{1,0:T(8,128)(2,1)S(1)}, bf16[256,1024]{1,0:T(8,128)(2,1)S(1)}, u32[]{:S(2)}, u32[]{:S(2)}) collective-permute-start(bf16[256,1024]{1,0:T(8,128)(2,1)S(1)} %fusion.15), channel_id=1, source_target_pairs={{0,2},{1,3},{2,0},{3,1},{4,6},{5,7},{6,4},{7,5},{8,10},{9,11},{10,... | collective-permute-start | bytes 1572872 | tf_op jit(solution)/shard_map/ppermute | solution.py:27
  235.9 9.2 %collective-permute-start.10 = (bf16[256,1024]{1,0:T(8,128)(2,1)S(1)}, bf16[256,1024]{1,0:T(8,128)(2,1)S(1)}, u32[]{:S(2)}, u32[]{:S(2)}) collective-permute-start(bf16[256,1024]{1,0:T(8,128)(2,1)S(1)} %fusion.10), channel_id=1, source_target_pairs={{0,2},{1,3},{2,0},{3,1},{4,6},{5,7},{6,4},{7,5},{8,10},{9,11},{10,... | collective-permute-start | bytes 1572872 | tf_op jit(solution)/shard_map/ppermute | solution.py:27
  245.3 14.9 %collective-permute-start.11 = (bf16[512,1024]{1,0:T(8,128)(2,1)S(1)}, bf16[512,1024]{1,0:T(8,128)(2,1)S(1)}, u32[]{:S(2)}, u32[]{:S(2)}) collective-permute-start(bf16[512,1024]{1,0:T(8,128)(2,1)S(1)} %pad_maximum_fusion.2), channel_id=1, source_target_pairs={{0,1},{1,0},{2,3},{3,2},{4,5},{5,4},{6,7},{7,6},{8,9},{9,8},{10,11... | collective-permute-start | bytes 3145736 | tf_op jit(solution)/shard_map/ppermute | solution.py:27
  289.7 32.9 %all-to-all-start.1 = ((bf16[8,2,57344]{2,1,0:T(2,128)(2,1)}), bf16[8,2,57344]{2,1,0:T(2,128)(2,1)S(1)}, u32[]{:S(2)}, u32[]{:S(2)}) async-start(bf16[8,2,57344]{2,1,0:T(2,128)(2,1)} %reshape.106), calls=%async_computation.1 | async-start | bytes 3670016 | tf_op jit(solution)/shard_map/all_to_all | solution.py:92
where the time goes:
time: 336 us; the launch traced here: 335 us
  waiting for transfers between devices  178 us (53%)
  blocking collectives  43.5 us (13%)
  starting transfers between devices  35.9 us (11%)
  other arithmetic  24.9 us (7%)
  local copies, waits for them, and re-layouts  24.4 us (7%)
  matrix products  24 us (7%)
  between operations  4.73 us (1%)
    ppermute x12, waiting for transfers between devices, partner_2(): return lax.ppermute(value, axis, pairs)  149 us
    psum x1, blocking collectives, body(): totals = lax.psum(expert_sums, 'fsdp')  43.5 us
    all_to_all x1, waiting for transfers between devices, body(): lax.all_to_all(update[None], 'fsdp', split_axis=1, concat_axis=0, tiled=T...  28.7 us
    ppermute x12, starting transfers between devices, partner_2(): return lax.ppermute(value, axis, pairs)  24.4 us
    unnamed x12, local copies, waits for them, and re-layouts  13.6 us
    dot_general x3, matrix products, body(): jnp.dot(current, poly, preferred_element_type=jnp.float32)  11.7 us
    unnamed x1, other arithmetic  11.4 us
    all_to_all x1, starting transfers between devices, body(): lax.all_to_all(outbound, 'fsdp', split_axis=0, concat_axis=1, tiled=True)[0]  7.31 us
  transfers between devices with their start and end apart: 14, of which 13 were waited for; matrix products, arithmetic and copies ran while one was open for 1% of the time, Pallas kernels for 0%

commit v1 on v0

v1 whole, which is shorter than its diff:
```python
import math

import jax
import jax.numpy as jnp
from jax import lax
from jax.sharding import PartitionSpec as P

coef_a = 3.4445
coef_b = -4.775
coef_c = 2.0315
epsilon = 1e-07
ITERS = 3


def mm(a, b):
    return jnp.dot(a, b, preferred_element_type=jnp.float32)


def body(gradients, owner):
    expert_count, local_rows, columns = gradients.shape
    fsdp_size = lax.axis_size("fsdp")
    rows = local_rows * fsdp_size
    share = fsdp_size // expert_count
    f32, bf16 = jnp.float32, jnp.bfloat16
    sums = jnp.sum(jnp.square(gradients.astype(f32)), axis=(1, 2))
    totals = lax.psum(sums, "fsdp")
    norms = jnp.sqrt(totals)
    scales = 1.0 / (norms + epsilon)

    def one(pair):
        g, scale = pair
        local = lax.dot_general(g, g, (((0,), (0,)), ((), ())), preferred_element_type=f32)
        raw = lax.psum(local.astype(bf16), "fsdp")
        gram = (raw.astype(f32) * (scale * scale)).astype(bf16)
        current = g
        for it in range(ITERS):
            gf = gram.astype(f32)
            poly = (coef_b * gf + coef_c * mm(gram, gram)).astype(bf16)
            nxt = coef_a * current.astype(f32) + mm(current, poly)
            if it == 0:
                nxt = nxt * scale
            if it < ITERS - 1:
                half = (coef_a * gf + mm(gram, poly)).astype(bf16)
                gram = (coef_a * half.astype(f32) + mm(poly, half)).astype(bf16)
                current = nxt.astype(bf16)
        return (math.sqrt(rows) * nxt).astype(bf16)

    if expert_count <= 2:
        updates = jnp.stack([one((gradients[e], scales[e])) for e in range(expert_count)])
    else:
        updates = lax.map(one, (gradients, scales))
    place = lax.axis_index("fsdp") // share
    mine = jnp.sum(jnp.where(owner[0] == place, norms, 0.0))
    slot_rms = (mine / math.sqrt(rows * columns)).reshape(1, 1)
    return updates, slot_rms


def solution(mesh):
    return jax.shard_map(
        body,
        mesh=mesh,
        in_specs=(P("expert", "fsdp", None), P("expert", None)),
        out_specs=(P("expert", "fsdp", None), P("expert", "fsdp")),
        check_vma=False,
    )
```

time: 336 us -> 249 us (0.74)
  waiting for transfers between devices: 178 us -> 130 us
  matrix products: 24 us -> 70.5 us
  starting transfers between devices: 35.9 us -> 0.04 us
  local copies, waits for them, and re-layouts: 24.4 us -> 0.61 us
  other arithmetic: 24.9 us -> 2.59 us
  blocking collectives: 43.5 us -> 23.6 us
  between operations: 4.73 us -> 18.9 us
    ppermute x12 -> x0, waiting for transfers between devices: 149 us -> none  [partner_2(): return lax.ppermute(value, axis, pairs)]
    psum x0 -> x1, waiting for transfers between devices: none -> 130 us  [one(): raw = lax.psum(local.astype(bf16), 'fsdp')]
    dot_general x8 -> x20, matrix products: 24 us -> 70.5 us  [the longest x18 63.7 us: mm(): return jnp.dot(a, b, preferred_element_type=jnp.float32)]
    all_to_all x2 -> x0, waiting for transfers between devices: 28.7 us -> none  [the longest x1 28.7 us: body(): lax.all_to_all(update[None], 'fsdp', split_axis=1, concat_axis=0, tiled=T...]
    ppermute x12 -> x0, starting transfers between devices: 24.4 us -> none  [partner_2(): return lax.ppermute(value, axis, pairs)]
    psum x1, blocking collectives: 43.5 us -> 23.6 us  [body(): totals = lax.psum(sums, 'fsdp')]
    unnamed x12, local copies, waits for them, and re-layouts: 13.6 us -> 0.02 us
    all_to_all x2 -> x0, starting transfers between devices: 11.5 us -> none  [the longest x1 7.31 us: body(): lax.all_to_all(outbound, 'fsdp', split_axis=0, concat_axis=1, tiled=True)[0]]
  transfers between devices with their start and end apart: 14 -> 1, of which waited for: 13 -> 1; matrix products, arithmetic and copies ran while one was open for 1% -> 1% of each run, Pallas kernels for 0% -> 0%
where the time goes in v1:
time: 249 us; the launch traced here: 246 us
  waiting for transfers between devices  130 us (52%)
  matrix products  70.5 us (28%)
  blocking collectives  23.6 us (9%)
  between operations  18.9 us (8%)
  other arithmetic  2.59 us (1%)
    psum x1, waiting for transfers between devices, one(): raw = lax.psum(local.astype(bf16), 'fsdp')  130 us
    dot_general x18, matrix products, mm(): return jnp.dot(a, b, preferred_element_type=jnp.float32)  63.7 us
    psum x1, blocking collectives, body(): totals = lax.psum(sums, 'fsdp')  23.6 us
    dot_general x2, matrix products, one(): lax.dot_general(g, g, (((0,), (0,)), ((), ())), preferred_element_type=f32)  6.82 us
  transfers between devices with their start and end apart: 1, of which 1 were waited for; matrix products, arithmetic and copies ran while one was open for 1% of the time, Pallas kernels for 0%

profile of v1, /device:TPU:0, one launch (start us, length us, event | category | flops | bytes accessed | tf_op | source)
XLA Modules:
  0.0 246.2 jit_solution(4956470677624949389)
XLA Ops:
  7.2 0.0 copy-start
  7.2 0.0 all-reduce.3.cloned.1.call-start
  7.2 4.2 %convolution_convert_fusion = bf16[1024,1024]{1,0:T(8,128)(2,1)} fusion(bf16[2,448,1024]{2,1,0:T(8,128)(2,1)} %param.2), kind=kOutput, calls=%fused_computation.35 | convolution fusion | flops 940572672 | bytes 3014656 | tf_op jit(solution)/shard_map/dot_general | solution.py:32
  11.4 0.0 copy-done
  11.4 2.6 %convolution_convert_fusion.1 = bf16[1024,1024]{1,0:T(8,128)(2,1)} fusion(bf16[2,448,1024]{2,1,0:T(8,128)(2,1)S(1)} %copy-done), kind=kOutput, calls=%fused_computation.36 | convolution fusion | flops 940572672 | bytes 3014656 | tf_op jit(solution)/shard_map/dot_general | solution.py:32
  14.0 0.0 copy-start.1
  14.0 0.0 all-reduce.3.cloned.1.call-update
  14.1 0.6 multiply_reduce_fusion
  14.7 23.6 %psum.22 = f32[2]{0:T(128)S(1)} all-reduce(f32[2]{0:T(128)S(1)} %multiply_reduce_fusion), channel_id=1, replica_groups=mesh['expert'=4,'fsdp'=8] {'fsdp'}, use_global_device_ids=true, to_apply=%region_2.0 | all-reduce | flops 2 | bytes 16 | tf_op jit(solution)/shard_map/psum | solution.py:26
  38.3 0.0 copy-done.1
  38.3 0.6 fusion.36
  38.9 0.6 fusion.47
  42.6 129.9 %all-reduce.3.cloned.1.call-done = (bf16[1024,1024]{1,0:T(8,128)(2,1)}, bf16[1024,1024]{1,0:T(8,128)(2,1)}) async-done(((bf16[1024,1024]{1,0:T(8,128)(2,1)}, bf16[1024,1024]{1,0:T(8,128)(2,1)}), (bf16[1024,1024]{1,0:T(8,128)(2,1)}, bf16[1024,1024]{1,0:T(8,128)(2,1)})) %all-reduce.3.cloned.1.call-update) | async-done | bytes 4194320 | tf_op jit(solution)/shard_map/psum | solution.py:33
  172.5 0.0 copy-start.3
  172.5 5.5 %fusion.1 = bf16[1024,1024]{1,0:T(8,128)(2,1)S(1)} fusion(f32[]{:T(128)S(6)} %mul.115, bf16[1024,1024]{1,0:T(8,128)(2,1)} %get-tuple-element.3), kind=kOutput, calls=%fused_computation.9 | convolution fusion | flops 2159017984 | bytes 4194308 | tf_op jit(solution)/shard_map/dot_general | solution.py:16
  178.1 0.0 copy-done.3
  178.1 2.3 fusion.24
  180.4 0.0 copy-start.2
  180.4 1.9 fusion.23
  182.4 0.0 copy-done.2
  182.4 2.6 %fusion.9 = bf16[1024,1024]{1,0:T(8,128)(2,1)S(1)} fusion(f32[]{:T(128)S(6)} %mul.134, bf16[1024,1024]{1,0:T(8,128)(2,1)S(1)} %copy-done.2), kind=kOutput, calls=%fused_computation.17 | convolution fusion | flops 2159017984 | bytes 4194308 | tf_op jit(solution)/shard_map/dot_general | solution.py:16
  185.0 2.3 fusion.25
  187.3 1.7 fusion.21
  189.0 2.7 %add_convert_fusion.5 = bf16[1024,1024]{1,0:T(8,128)(2,1)S(1)} fusion(bf16[1024,1024]{1,0:T(8,128)(2,1)S(1)} %fusion.1, f32[1024,1024]{1,0:T(8,128)S(1)} %fusion.24, f32[]{:T(128)S(6)} %mul.115, bf16[1024,1024]{1,0:T(8,128)(2,1)S(1)} %copy-done.3), kind=kOutput, calls=%fused_computation.30 | convolution fusion | flops 2166358016 | bytes 10485764 | tf_op jit(solution)/shard_map/dot_general | solution.py:16
  191.8 2.7 %fusion.5 = bf16[1024,1024]{1,0:T(8,128)(2,1)S(1)} fusion(bf16[1024,1024]{1,0:T(8,128)(2,1)S(1)} %add_convert_fusion.5), kind=kOutput, calls=%fused_computation.13 | convolution fusion | flops 2152726528 | bytes 4194304 | tf_op jit(solution)/shard_map/dot_general | solution.py:16
  194.5 2.4 fusion.7
  196.8 0.0 copy-start.4
  196.8 4.3 %fusion.48 = f32[1024,1024]{1,0:T(8,128)} fusion(bf16[1024,1024]{1,0:T(8,128)(2,1)S(1)} %fusion.5, bf16[1024,1024]{1,0:T(8,128)(2,1)S(1)} %fusion.7), kind=kOutput, calls=%fused_computation.72 | convolution fusion | flops 2147483648 | bytes 8388608 | tf_op jit(solution)/shard_map/dot_general | solution.py:16
  201.1 0.0 copy-done.4
  201.1 1.2 add_convert_fusion.9
  202.3 2.7 %add_convert_fusion.2 = bf16[1024,1024]{1,0:T(8,128)(2,1)S(1)} fusion(bf16[1024,1024]{1,0:T(8,128)(2,1)S(1)} %fusion.9, f32[1024,1024]{1,0:T(8,128)S(1)} %fusion.25, f32[]{:T(128)S(6)} %mul.134, bf16[1024,1024]{1,0:T(8,128)(2,1)S(1)} %copy-done.2), kind=kOutput, calls=%fused_computation.26 | convolution fusion | flops 2166358016 | bytes 10485764 | tf_op jit(solution)/shard_map/dot_general | solution.py:16
  205.1 2.5 fusion.13
  207.5 2.6 %fusion.15 = bf16[1024,1024]{1,0:T(8,128)(2,1)S(1)} fusion(bf16[1024,1024]{1,0:T(8,128)(2,1)S(1)} %add_convert_fusion.2, bf16[1024,1024]{1,0:T(8,128)(2,1)S(1)} %fusion.13), kind=kOutput, calls=%fused_computation.23 | convolution fusion | flops 2151677952 | bytes 6291456 | tf_op jit(solution)/shard_map/dot_general | solution.py:16
  210.1 0.0 copy-start.5
  210.1 4.3 %fusion.49 = f32[1024,1024]{1,0:T(8,128)} fusion(bf16[1024,1024]{1,0:T(8,128)(2,1)S(1)} %fusion.13, bf16[1024,1024]{1,0:T(8,128)(2,1)S(1)} %fusion.15), kind=kOutput, calls=%fused_computation.73 | convolution fusion | flops 2147483648 | bytes 8388608 | tf_op jit(solution)/shard_map/dot_general | solution.py:16
  214.4 0.0 copy-done.5
  214.4 1.2 add_convert_fusion.8
  215.6 10.5 %fusion.26 = bf16[1,448,1024]{2,1,0:T(8,128)(2,1)S(1)} fusion(bf16[448,1024]{1,0:T(8,128)(2,1)S(1)} %add_convert_fusion.9, f32[1024,1024]{1,0:T(8,128)} %fusion.48, bf16[1024,1024]{1,0:T(8,128)(2,1)} %copy-done.4), kind=kOutput, calls=%fused_computation.50 | convolution fusion | flops 3102932992 | bytes 8126464 | tf_op jit(solution)/shard_map/dot_general | solution.py:16
  226.1 10.3 %fusion.27 = bf16[1,448,1024]{2,1,0:T(8,128)(2,1)S(1)} fusion(bf16[448,1024]{1,0:T(8,128)(2,1)S(1)} %add_convert_fusion.8, f32[1024,1024]{1,0:T(8,128)} %fusion.49, bf16[1024,1024]{1,0:T(8,128)(2,1)} %copy-done.5), kind=kOutput, calls=%fused_computation.51 | convolution fusion | flops 3102932992 | bytes 8126464 | tf_op jit(solution)/shard_map/dot_general | solution.py:16
  236.4 1.4 pad_maximum_fusion
Async XLA Ops:
  7.2 4.3 %copy-start = (bf16[2,448,1024]{2,1,0:T(8,128)(2,1)S(1)}, bf16[2,448,1024]{2,1,0:T(8,128)(2,1)}, u32[]{:S(2)}) copy-start(bf16[2,448,1024]{2,1,0:T(8,128)(2,1)} %param.2) | copy-start | bytes 5505028
  7.2 165.4 %all-reduce.3.cloned.1.call-start = ((), (), s32[]{:S(2)}) async-start(), calls=%async_computation | async-start | bytes 8388608 | tf_op jit(solution)/shard_map/psum | solution.py:33
  14.0 24.3 %copy-start.1 = (s32[1,2]{1,0:T(1,128)S(1)}, s32[1,2]{1,0:T(1,128)}, u32[]{:S(2)}) copy-start(s32[1,2]{1,0:T(1,128)} %param.3) | copy-start | bytes 28
  172.5 5.5 %copy-start.3 = (bf16[1024,1024]{1,0:T(8,128)(2,1)S(1)}, bf16[1024,1024]{1,0:T(8,128)(2,1)}, u32[]{:S(2)}) copy-start(bf16[1024,1024]{1,0:T(8,128)(2,1)} %get-tuple-element.3) | copy-start | bytes 6291460
  180.4 2.0 copy-start.2
  196.8 4.3 %copy-start.4 = (bf16[1024,1024]{1,0:T(8,128)(2,1)}, bf16[1024,1024]{1,0:T(8,128)(2,1)S(1)}, u32[]{:S(2)}) copy-start(bf16[1024,1024]{1,0:T(8,128)(2,1)S(1)} %fusion.7) | copy-start | bytes 6291460
  210.1 4.3 %copy-start.5 = (bf16[1024,1024]{1,0:T(8,128)(2,1)}, bf16[1024,1024]{1,0:T(8,128)(2,1)S(1)}, u32[]{:S(2)}) copy-start(bf16[1024,1024]{1,0:T(8,128)(2,1)S(1)} %fusion.15) | copy-start | bytes 6291460
Sparse Core Ops, SparseCore 0:
  14.2 158.3 all-reduce.2

commit v2 on v1

--- a/solution.py
+++ b/solution.py
@@ -1,8 +1,11 @@
+import functools
 import math
 
 import jax
 import jax.numpy as jnp
 from jax import lax
+from jax.experimental import pallas as pl
+from jax.experimental.pallas import tpu as pltpu
 from jax.sharding import PartitionSpec as P
 
 coef_a = 3.4445
@@ -10,21 +13,248 @@
 coef_c = 2.0315
 epsilon = 1e-07
 ITERS = 3
+MESH = pl.DeviceIdType.MESH
+f32, bf16 = jnp.float32, jnp.bfloat16
 
 
 def mm(a, b):
-    return jnp.dot(a, b, preferred_element_type=jnp.float32)
-
-
-def body(gradients, owner):
-    expert_count, local_rows, columns = gradients.shape
-    fsdp_size = lax.axis_size("fsdp")
-    rows = local_rows * fsdp_size
-    share = fsdp_size // expert_count
-    f32, bf16 = jnp.float32, jnp.bfloat16
+    return jnp.dot(a, b, preferred_element_type=f32)
+
+
+def kernel(rows, g_ref, out_ref, norm_ref, part, xr, pair, zr, red, gram, poly, half, ping, pong, nb,
+           n_send, n_recv, xs_send, xs_recv, zs_send, zs_recv, za_send, za_recv, xa_send, xa_recv):
+    experts, local_rows, columns = g_ref.shape
+    tile = columns // 4
+    piece = tile // 4
+    blocks = [(i, j) for i in range(4) for j in range(i, 4)]
+    per = len(blocks) // 2
+    chunks = experts * per
+    size = lax.axis_size("fsdp")
+    me = lax.axis_index("fsdp")
+    z, x = me // 2, me % 2
+    partner = z * 2 + (1 - x)
+
+    barrier = pltpu.get_barrier_semaphore()
+    for d in range(1, size):
+        pl.semaphore_signal(barrier, inc=1, device_id={"fsdp": (me + d) % size}, device_id_type=MESH)
+
+    def remote(src, dst, send, recv, peer):
+        return pltpu.make_async_remote_copy(
+            src_ref=src, dst_ref=dst, send_sem=send, recv_sem=recv, device_id={"fsdp": peer}, device_id_type=MESH
+        )
+
+    def local_gram(e):
+        for i in range(4):
+            strip = lax.dot_general(
+                g_ref[e, :, tile * i:tile * (i + 1)], g_ref[e, :, tile * i:], (((0,), (0,)), ((), ())),
+                preferred_element_type=f32,
+            ).astype(bf16)
+            for j in range(i, 4):
+                part[e, blocks.index((i, j))] = strip[:, tile * (j - i):tile * (j - i + 1)]
+
+    def squares(e):
+        total = jnp.zeros((8, 128), f32)
+        for n in range(columns // 128):
+            value = g_ref[e, :, 128 * n:128 * (n + 1)].astype(f32)
+            total = total + jnp.sum((value * value).reshape(local_rows // 8, 8, 128), axis=0)
+        nb[0, e] = total
+
+    def x_scatter(k):
+        e, c = divmod(k, per)
+        return remote(part.at[e, per * (1 - x) + c], xr.at[k], xs_send.at[k], xs_recv.at[k], partner)
+
+    def z_peer(d):
+        return (z + d) % 4
+
+    def z_scatter(k, d):
+        rows_of = pl.ds(pl.multiple_of(z_peer(d) * piece, piece), piece)
+        return remote(pair.at[k, rows_of], zr.at[k, d - 1], zs_send.at[k, d - 1], zs_recv.at[k, d - 1],
+                      z_peer(d) * 2 + x)
+
+    mine = pl.ds(pl.multiple_of(z * piece, piece), piece)
+
+    def z_gather(k, d):
+        e, c = divmod(k, per)
+        slot = red.at[e, per * x + c, mine]
+        return remote(slot, slot, za_send.at[k, d - 1], za_recv.at[k, d - 1], z_peer(d) * 2 + x)
+
+    def x_gather(k):
+        e, c = divmod(k, per)
+        slot = red.at[e, per * x + c]
+        return remote(slot, slot, xa_send.at[k], xa_recv.at[k], partner)
+
+    def step_b(k):
+        e, c = divmod(k, per)
+        x_scatter(k).wait_recv()
+        pair[k] = (part[e, per * x + c].astype(f32) + xr[k].astype(f32)).astype(bf16)
+        for d in (2, 1, 3):
+            z_scatter(k, d).start()
+
+    def step_c(k):
+        e, c = divmod(k, per)
+        total = pair[k, mine].astype(f32)
+        for d in (1, 2, 3):
+            z_scatter(k, d).wait_recv()
+            total = total + zr[k, d - 1].astype(f32)
+        red[e, per * x + c, mine] = total.astype(bf16)
+        for d in (2, 1, 3):
+            z_gather(k, d).start()
+
+    def step_d(k):
+        for d in (1, 2, 3):
+            z_gather(k, d).wait_recv()
+        x_gather(k).start()
+        if k + per < chunks:
+            x_scatter(k + per).start()
+
+    def unpack(e, scale):
+        for c in range(per):
+            x_gather(e * per + c).wait_recv()
+        for b, (i, j) in enumerate(blocks):
+            block = red[e, b].astype(f32) * (scale * scale)
+            gram[tile * i:tile * (i + 1), tile * j:tile * (j + 1)] = block.astype(bf16)
+            if i != j:
+                gram[tile * j:tile * (j + 1), tile * i:tile * (i + 1)] = block.T.astype(bf16)
+
+    def by_columns(fn):
+        def step(n, carry):
+            fn(pl.ds(pl.multiple_of(n * tile, tile), tile))
+            return carry
+        lax.fori_loop(0, 4, step, 0)
+
+    def stage_poly():
+        def fn(cols):
+            poly[:, cols] = (coef_b * gram[:, cols].astype(f32) + coef_c * mm(gram[...], gram[:, cols])).astype(bf16)
+        by_columns(fn)
+
+    def stage_half():
+        def fn(cols):
+            half[:, cols] = (coef_a * gram[:, cols].astype(f32) + mm(gram[...], poly[:, cols])).astype(bf16)
+        by_columns(fn)
+
+    def stage_gram():
+        def fn(cols):
+            gram[:, cols] = (coef_a * half[:, cols].astype(f32) + mm(poly[...], half[:, cols])).astype(bf16)
+        by_columns(fn)
+
+    def stage_rows(src, dst, factor):
+        def fn(cols):
+            value = coef_a * src[:, cols].astype(f32) + mm(src[...], poly[:, cols])
+            if factor is not None:
+                value = value * factor
+            dst[:, cols] = value.astype(bf16)
+        by_columns(fn)
+
+    def stages(e, scale):
+        root = math.sqrt(rows)
+        return [
+            functools.partial(unpack, e, scale),
+            stage_poly, stage_half, stage_gram,
+            functools.partial(stage_rows, g_ref.at[e], ping, scale),
+            stage_poly, stage_half, stage_gram,
+            functools.partial(stage_rows, ping, pong, None),
+            stage_poly,
+            functools.partial(stage_rows, pong, out_ref.at[e], root),
+        ]
+
+    local_gram(0)
+    pl.semaphore_wait(barrier, size - 1)
+    for k in range(per):
+        x_scatter(k).start()
+    for e in range(experts):
+        squares(e)
+
+    def norm_copy(d):
+        return remote(nb.at[0], nb.at[d], n_send.at[d - 1], n_recv.at[d - 1], (me + d) % size)
+
+    for d in range(1, size):
+        norm_copy(d).start()
+    local_gram(1)
+
+    scales = []
+
+    def finish_norms():
+        total = nb[0]
+        for d in range(1, size):
+            norm_copy(d).wait_recv()
+            total = total + nb[d]
+        for e in range(experts):
+            norm = jnp.sqrt(jnp.sum(total[e], keepdims=True))
+            norm_ref[e] = jnp.broadcast_to(norm, (8, 128))
+            scales.append(1.0 / (norm + epsilon))
+
+    work = []
+    for t in range(chunks + 2):
+        if t < chunks:
+            step_b(t)
+        if 0 <= t - 1 < chunks:
+            step_c(t - 1)
+        if 0 <= t - 2 < chunks:
+            step_d(t - 2)
+        if t == per:
+            finish_norms()
+            work = stages(0, scales[0])
+        if t >= per + 2:
+            for _ in range(3):
+                if work:
+                    work.pop(0)()
+    while work:
+        work.pop(0)()
+    for stage in stages(1, scales[1]):
+        stage()
+
+    for k in range(chunks):
+        x_scatter(k).wait_send()
+        x_gather(k).wait_send()
+        for d in (1, 2, 3):
+            z_scatter(k, d).wait_send()
+            z_gather(k, d).wait_send()
+    for d in range(1, size):
+        norm_copy(d).wait_send()
+
+
+def fused(gradients, rows):
+    experts, local_rows, columns = gradients.shape
+    tile = columns // 4
+    chunks = experts * 5
+    dma = pltpu.SemaphoreType.DMA
+    vmem = pl.BlockSpec(memory_space=pltpu.VMEM)
+    return pl.pallas_call(
+        functools.partial(kernel, rows),
+        out_shape=(
+            jax.ShapeDtypeStruct(gradients.shape, bf16),
+            jax.ShapeDtypeStruct((experts, 8, 128), f32),
+        ),
+        in_specs=[vmem],
+        out_specs=(vmem, vmem),
+        scratch_shapes=[
+            pltpu.VMEM((experts, 10, tile, tile), bf16),
+            pltpu.VMEM((chunks, tile, tile), bf16),
+            pltpu.VMEM((chunks, tile, tile), bf16),
+            pltpu.VMEM((chunks, 3, tile // 4, tile), bf16),
+            pltpu.VMEM((experts, 10, tile, tile), bf16),
+            pltpu.VMEM((columns, columns), bf16),
+            pltpu.VMEM((columns, columns), bf16),
+            pltpu.VMEM((columns, columns), bf16),
+            pltpu.VMEM((local_rows, columns), bf16),
+            pltpu.VMEM((local_rows, columns), bf16),
+            pltpu.VMEM((8, experts, 8, 128), f32),
+            dma((7,)), dma((7,)),
+            dma((chunks,)), dma((chunks,)),
+            dma((chunks, 3)), dma((chunks, 3)),
+            dma((chunks, 3)), dma((chunks, 3)),
+            dma((chunks,)), dma((chunks,)),
+        ],
+        compiler_params=pltpu.CompilerParams(
+            collective_id=0, has_side_effects=True, vmem_limit_bytes=60 * 1024 * 1024
+        ),
+    )(gradients)
+
+
+def general(gradients, rows):
+    expert_count = gradients.shape[0]
     sums = jnp.sum(jnp.square(gradients.astype(f32)), axis=(1, 2))
-    totals = lax.psum(sums, "fsdp")
-    norms = jnp.sqrt(totals)
+    norms = jnp.sqrt(lax.psum(sums, "fsdp"))
     scales = 1.0 / (norms + epsilon)
 
     def one(pair):
@@ -45,10 +275,19 @@
                 current = nxt.astype(bf16)
         return (math.sqrt(rows) * nxt).astype(bf16)
 
-    if expert_count <= 2:
-        updates = jnp.stack([one((gradients[e], scales[e])) for e in range(expert_count)])
+    return lax.map(one, (gradients, scales)), norms
+
+
+def body(gradients, owner):
+    expert_count, local_rows, columns = gradients.shape
+    fsdp_size = lax.axis_size("fsdp")
+    rows = local_rows * fsdp_size
+    share = fsdp_size // expert_count
+    if fsdp_size == 8 and expert_count == 2 and columns % 1024 == 0 and local_rows % 16 == 0:
+        updates, norm_tiles = fused(gradients, rows)
+        norms = norm_tiles[:, 0, 0]
     else:
-        updates = lax.map(one, (gradients, scales))
+        updates, norms = general(gradients, rows)
     place = lax.axis_index("fsdp") // share
     mine = jnp.sum(jnp.where(owner[0] == place, norms, 0.0))
     slot_rms = (mine / math.sqrt(rows * columns)).reshape(1, 1)

time: 249 us -> 123 us (0.49)
  waiting for transfers between devices: 130 us -> 0 us
  Pallas kernels: 0 us -> 116 us
  matrix products: 70.5 us -> 0 us
  blocking collectives: 23.6 us -> 0 us
  between operations: 18.9 us -> 2.44 us
  local copies, waits for them, and re-layouts: 0.61 us -> 3.67 us
    psum x1 -> x0, waiting for transfers between devices: 130 us -> none  [one(): raw = lax.psum(local.astype(bf16), 'fsdp')]
    pallas_call x0 -> x1, Pallas kernels: none -> 116 us  [fused(): pl.pallas_call(functools.partial(kernel, rows), out_shape=(jax.ShapeDtype...]
    dot_general x20 -> x0, matrix products: 70.5 us -> none  [the longest x18 63.7 us: mm(): return jnp.dot(a, b, preferred_element_type=jnp.float32)]
    psum x1 -> x0, blocking collectives: 23.6 us -> none  [body(): totals = lax.psum(sums, 'fsdp')]
    unnamed x12 -> x3, local copies, waits for them, and re-layouts: 0.02 us -> 2.88 us
  transfers between devices with their start and end apart: 1 -> 0, of which waited for: 1 -> 0; matrix products, arithmetic and copies ran while one was open for 1% -> 0% of each run, Pallas kernels for 0% -> 0%
where the time goes in v2:
time: 123 us
  Pallas kernels  116 us (94%)
  local copies, waits for them, and re-layouts  3.67 us (3%)
  between operations  2.44 us (2%)
    pallas_call x1, Pallas kernels, fused(): pl.pallas_call(functools.partial(kernel, rows), out_shape=(jax.ShapeDtype...  116 us
    unnamed x3, local copies, waits for them, and re-layouts  2.88 us

profile of v2, /device:TPU:0, one launch (start us, length us, event | category | flops | bytes accessed | tf_op | source)
XLA Modules:
  0.0 122.5 jit_solution(7075476168607352559)
XLA Ops:
  0.6 0.0 copy-start
  0.7 115.8 %shard_map.41 = (bf16[2,448,1024]{2,1,0:T(8,128)(2,1)}, f32[2,8,128]{2,1,0:T(8,128)}) custom-call(bf16[2,448,1024]{2,1,0:T(8,128)(2,1)} %g_ref.1), custom_call_target="tpu_custom_call" | custom-call | tf_op jit(solution)/shard_map/pallas_call | solution.py:222
  116.5 0.8 slice_reduce_fusion
  117.3 0.0 copy-done
  117.3 0.6 fusion
  118.5 2.9 %copy.5 = bf16[2,448,1024]{2,1,0:T(8,128)(2,1)} copy(bf16[2,448,1024]{2,1,0:T(8,128)(2,1)} %get-tuple-element.8) | data formatting | bytes 3670016
Async XLA Ops:
  0.6 116.7 %copy-start = (s32[1,2]{1,0:T(1,128)S(1)}, s32[1,2]{1,0:T(1,128)}, u32[]{:S(2)}) copy-start(s32[1,2]{1,0:T(1,128)} %param.3) | copy-start | bytes 28

commit v3 on v2

--- a/solution.py
+++ b/solution.py
@@ -116,34 +116,31 @@
             if i != j:
                 gram[tile * j:tile * (j + 1), tile * i:tile * (i + 1)] = block.T.astype(bf16)
 
-    def by_columns(fn):
-        def step(n, carry):
-            fn(pl.ds(pl.multiple_of(n * tile, tile), tile))
-            return carry
-        lax.fori_loop(0, 4, step, 0)
+    def mirrored(dst, fn):
+        for j in range(4):
+            cols = slice(tile * j, tile * (j + 1))
+            value = fn(tile * (j + 1), cols)
+            dst[:tile * (j + 1), cols] = value.astype(bf16)
+            for i in range(j):
+                span = slice(tile * i, tile * (i + 1))
+                dst[cols, span] = value[span].astype(bf16).T
 
     def stage_poly():
-        def fn(cols):
-            poly[:, cols] = (coef_b * gram[:, cols].astype(f32) + coef_c * mm(gram[...], gram[:, cols])).astype(bf16)
-        by_columns(fn)
+        mirrored(poly, lambda m, cols: coef_b * gram[:m, cols].astype(f32) + coef_c * mm(gram[:m], gram[:, cols]))
 
     def stage_half():
-        def fn(cols):
-            half[:, cols] = (coef_a * gram[:, cols].astype(f32) + mm(gram[...], poly[:, cols])).astype(bf16)
-        by_columns(fn)
+        mirrored(half, lambda m, cols: coef_a * gram[:m, cols].astype(f32) + mm(gram[:m], poly[:, cols]))
 
     def stage_gram():
-        def fn(cols):
-            gram[:, cols] = (coef_a * half[:, cols].astype(f32) + mm(poly[...], half[:, cols])).astype(bf16)
-        by_columns(fn)
+        mirrored(gram, lambda m, cols: coef_a * half[:m, cols].astype(f32) + mm(poly[:m], half[:, cols]))
 
     def stage_rows(src, dst, factor):
-        def fn(cols):
+        for n in range(2):
+            cols = slice(2 * tile * n, 2 * tile * (n + 1))
             value = coef_a * src[:, cols].astype(f32) + mm(src[...], poly[:, cols])
             if factor is not None:
                 value = value * factor
             dst[:, cols] = value.astype(bf16)
-        by_columns(fn)
 
     def stages(e, scale):
         root = math.sqrt(rows)

time: 123 us -> 106 us (0.86)
  Pallas kernels: 116 us -> 99 us
    pallas_call x1, Pallas kernels: 116 us -> 99 us  [fused(): pl.pallas_call(functools.partial(kernel, rows), out_shape=(jax.ShapeDtype...]
where the time goes in v3:
time: 106 us
  Pallas kernels  99 us (93%)
  local copies, waits for them, and re-layouts  3.67 us (3%)
  between operations  2.44 us (2%)
    pallas_call x1, Pallas kernels, fused(): pl.pallas_call(functools.partial(kernel, rows), out_shape=(jax.ShapeDtype...  99 us
    unnamed x3, local copies, waits for them, and re-layouts  2.88 us

profile of v3, /device:TPU:0, one launch (start us, length us, event | category | flops | bytes accessed | tf_op | source)
XLA Modules:
  0.0 105.7 jit_solution(589752188208947415)
XLA Ops:
  0.6 0.0 copy-start
  0.7 99.0 %shard_map.41 = (bf16[2,448,1024]{2,1,0:T(8,128)(2,1)}, f32[2,8,128]{2,1,0:T(8,128)}) custom-call(bf16[2,448,1024]{2,1,0:T(8,128)(2,1)} %g_ref.1), custom_call_target="tpu_custom_call" | custom-call | tf_op jit(solution)/shard_map/pallas_call | solution.py:219
  99.6 0.8 slice_reduce_fusion
  100.4 0.0 copy-done
  100.4 0.6 fusion
  101.7 2.9 %copy.5 = bf16[2,448,1024]{2,1,0:T(8,128)(2,1)} copy(bf16[2,448,1024]{2,1,0:T(8,128)(2,1)} %get-tuple-element.8) | data formatting | bytes 3670016
Async XLA Ops:
  0.6 99.8 %copy-start = (s32[1,2]{1,0:T(1,128)S(1)}, s32[1,2]{1,0:T(1,128)}, u32[]{:S(2)}) copy-start(s32[1,2]{1,0:T(1,128)} %param.3) | copy-start | bytes 28
